TPU v7x, 32 devices: a whole 2x2x4 slice. The times are simulated.
32 devices in a mesh: group: 2 (over y), tm: 4 (over z), bl: 2 (over x), pol: 2 (over core).
Axes of the slice: x: 2, y: 2, z: 4, core: 2. Of those that a mesh axis runs over, the one named last changes fastest.
Arguments:
- visibilities: bfloat16 [1600, 256, 2, 384], P(('group', 'tm'), ('bl', 'pol')), parts along dimension 0, may hold values from -6 to 6
- flag_mask: int32 [1600], P(('group', 'tm')), parts along dimension 0, may hold values 0 or 1
- kernel_index: int32 [256], P(('bl', 'pol')), may hold values from 0 to 15
- filter_bank: float32 [2, 16, 257], replicated, may hold values from -0.875 to 0.875
Outputs:
- fringe_filtered: bfloat16 [160, 256, 2, 384], P('group', ('bl', 'pol', 'tm')), parts along dimension 0
There are 2 independent parts, one for each index of `group`. A program takes and returns all parts, laid end to end along the dimension named above; an argument that names none is the same for every part. Nothing has to cross between parts.
All inputs are finite; a program needn't handle non-finite values. No bound on the sum of `flag_mask` on one device may be relied on, other than what follows from the above.
Results may differ from a plain program's by a relative error of at most 0.001.
Values may be sent and summed in bfloat16 or wider, within the bound.
No kernel may reach another device: no remote copies, remote signals or barrier semaphores. Data moves between devices by JAX's collectives and lax.ppermute only.
A program may use at most 192 MiB of HBM per device.

v0:
```python
import jax
import jax.numpy as jnp
from jax import lax
from jax.sharding import PartitionSpec as P

TAPS = 257
AVG = 10


def padded(block, sides, width):
    for axis, dim in sides:
        count = lax.axis_size(axis)
        forward = [(i, i + 1) for i in range(count - 1)]
        backward = [(target, source) for source, target in forward]
        low = lax.ppermute(
            lax.slice_in_dim(block, block.shape[dim] - width, None, axis=dim), axis, forward
        )
        high = lax.ppermute(lax.slice_in_dim(block, 0, width, axis=dim), axis, backward)
        block = jnp.concatenate([low, block, high], axis=dim)
    return block


def select_taps(kernel_index, filter_bank):
    choices_count = filter_bank.shape[1]
    one_hot = (kernel_index[:, None] == jnp.arange(choices_count, dtype=jnp.int32)[None, :]).astype(
        jnp.float32
    )
    return jnp.einsum("bk,rkt->brt", one_hot, filter_bank, precision=lax.Precision.HIGHEST)


def make_band(kernel_taps, block_rows):
    tap_count = kernel_taps.shape[1]
    row_width = block_rows + tap_count - 1
    zero_tail = jnp.zeros((2, block_rows), jnp.float32)
    period_row = jnp.concatenate([kernel_taps, zero_tail], axis=1)
    tiled_rows = jnp.tile(period_row, (1, block_rows))[:, : block_rows * row_width]
    return tiled_rows.reshape(2, block_rows, row_width)


def filter_block(time_slab, kernel_taps, block_rows):
    band_rows = make_band(kernel_taps, block_rows)
    row_width = band_rows.shape[2]
    band_rows = band_rows.reshape(2, block_rows // AVG, AVG, row_width).sum(axis=2) * (1.0 / AVG)
    out_count = band_rows.shape[1]
    stacked = band_rows.reshape(2 * out_count, row_width)
    product = jnp.dot(
        stacked, time_slab, precision=lax.Precision.HIGHEST, preferred_element_type=jnp.float32
    )
    prod_real = product[:out_count]
    prod_imag = product[out_count:]
    channels = time_slab.shape[1] // 2
    out_real = prod_real[:, :channels] - prod_imag[:, channels:]
    out_imag = prod_real[:, channels:] + prod_imag[:, :channels]
    result = jnp.stack([out_real, out_imag], axis=1)
    return result


def per_device(visibilities, flag_mask, kernel_index, filter_bank):
    half_taps = TAPS // 2
    block_rows = visibilities.shape[0]
    masked = visibilities * flag_mask.astype(jnp.bfloat16)[:, None, None, None]
    extended = padded(masked, (("tm", 0),), half_taps)
    taps_all = select_taps(kernel_index, filter_bank)

    def per_base(base_index):
        time_slab = lax.dynamic_index_in_dim(extended, base_index, 1, False).astype(jnp.float32)
        time_slab = time_slab.reshape(extended.shape[0], -1)
        kernel_taps = lax.dynamic_index_in_dim(taps_all, base_index, 0, False)
        return filter_block(time_slab, kernel_taps, block_rows)

    filtered = lax.map(per_base, jnp.arange(visibilities.shape[1], dtype=jnp.int32))
    averaged = jnp.moveaxis(filtered, 0, 1).astype(jnp.bfloat16)
    return lax.all_to_all(averaged, "tm", split_axis=1, concat_axis=0, tiled=True)


def solution(mesh):
    placed = (
        P(("group", "tm"), ("bl", "pol"), None, None),
        P(("group", "tm")),
        P(("bl", "pol")),
        P(),
    )
    return jax.shard_map(
        per_device,
        mesh=mesh,
        in_specs=placed,
        out_specs=P("group", ("bl", "pol", "tm"), None, None),
        check_vma=False,
    )
```

profile of v0, /device:TPU:0, one launch (start us, length us, event | category | flops | bytes accessed | tf_op | source)
XLA Modules:
  0.0 985.1 jit_solution(15027337351065907888)
XLA Ops:
  0.7 25.5 %broadcast_multiply_fusion.1 = bf16[200,64,2,384]{3,2,1,0:T(2,128)(2,1)S(1)} fusion(bf16[200,64,2,384]{3,2,1,0:T(2,128)(2,1)} %param.6, bf16[200]{0:T(256)(128)(2,1)S(1)} %convert_element_type.11), kind=kLoop, calls=%fused_computation.11 | loop fusion | flops 9830400 | bytes 39322000 | tf_op jit(solution)/shard_map/mul | solution.py:61
  26.2 23.1 %fusion.6 = (bf16[128,64,2,384]{3,2,1,0:T(2,128)(2,1)}, bf16[128,64,2,384]{3,2,1,0:T(2,128)(2,1)}) fusion(bf16[200,64,2,384]{3,2,1,0:T(2,128)(2,1)S(1)} %broadcast_multiply_fusion.1), kind=kLoop, calls=%fused_computation.17 | loop fusion | bytes 50331648 | tf_op jit(solution)/shard_map/slice | solution.py:16
  49.3 9.5 collective-permute-start
  60.4 263.7 %collective-permute-done = bf16[128,64,2,384]{3,2,1,0:T(2,128)(2,1)} collective-permute-done((bf16[128,64,2,384]{3,2,1,0:T(2,128)(2,1)}, bf16[128,64,2,384]{3,2,1,0:T(2,128)(2,1)}, u32[]{:S(2)}, u32[]{:S(2)}) %collective-permute-start) | collective-permute-done | bytes 12582944 | tf_op jit(solution)/shard_map/ppermute | solution.py:15
  324.2 8.7 collective-permute-done.1
  332.8 69.3 %pad_maximum_fusion = bf16[456,64,2,384]{3,2,1,0:T(2,128)(2,1)} fusion(bf16[128,64,2,384]{3,2,1,0:T(2,128)(2,1)} %collective-permute-done.1, bf16[200,64,2,384]{3,2,1,0:T(2,128)(2,1)} %copy-done.2, bf16[128,64,2,384]{3,2,1,0:T(2,128)(2,1)} %collective-permute-done), kind=kLoop, calls=%fused_computation.10 | loop fusion | flops 44826624 | bytes 89653248 | tf_op jit(solution)/shard_map/concatenate | solution.py:19
  402.2 532.0 %while.10 = (s32[]{:T(128)}, bf16[64,20,2,384]{3,2,1,0:T(2,128)(2,1)}, s32[64]{0:T(128)S(1)}, f32[64,2,257]{2,0,1:T(8,128)S(1)}, bf16[456,64,2,384]{3,2,1,0:T(2,...) while((s32[]{:T(128)}, bf16[64,20,2,384]{3,2,1,0:T(2,128)(2,1)}, s32[64]{0:T(128)S(1)}, ...), condition=%wide.region_2.3_spmd, body=%wide.region_0.2_spmd.sunk | while | flops 168328320 | bytes 10199059 | solution.py:71
  407.7 1.6 constant_dynamic-slice_fusion.5
  416.0 1.6 constant_dynamic-slice_fusion.5
  424.3 1.6 constant_dynamic-slice_fusion.5
  432.6 1.6 constant_dynamic-slice_fusion.5
  440.9 1.6 constant_dynamic-slice_fusion.5
  449.2 1.6 constant_dynamic-slice_fusion.5
  457.5 1.6 constant_dynamic-slice_fusion.5
  465.8 1.6 constant_dynamic-slice_fusion.5
  474.1 1.6 constant_dynamic-slice_fusion.5
  482.5 1.6 constant_dynamic-slice_fusion.5
  490.8 1.6 constant_dynamic-slice_fusion.5
  499.1 1.6 constant_dynamic-slice_fusion.5
  507.4 1.6 constant_dynamic-slice_fusion.5
  515.7 1.6 constant_dynamic-slice_fusion.5
  524.0 1.6 constant_dynamic-slice_fusion.5
  532.3 1.6 constant_dynamic-slice_fusion.5
  540.6 1.6 constant_dynamic-slice_fusion.5
  549.0 1.6 constant_dynamic-slice_fusion.5
  557.3 1.6 constant_dynamic-slice_fusion.5
  565.6 1.6 constant_dynamic-slice_fusion.5
  573.9 1.6 constant_dynamic-slice_fusion.5
  582.2 1.6 constant_dynamic-slice_fusion.5
  590.5 1.6 constant_dynamic-slice_fusion.5
  598.8 1.6 constant_dynamic-slice_fusion.5
  607.1 1.6 constant_dynamic-slice_fusion.5
  615.4 1.6 constant_dynamic-slice_fusion.5
  623.8 1.6 constant_dynamic-slice_fusion.5
  632.1 1.6 constant_dynamic-slice_fusion.5
  640.4 1.6 constant_dynamic-slice_fusion.5
  740.1 1.6 constant_dynamic-slice_fusion.5
  748.4 1.6 constant_dynamic-slice_fusion.5
  756.7 1.6 constant_dynamic-slice_fusion.5
  765.1 1.6 constant_dynamic-slice_fusion.5
  773.4 1.6 constant_dynamic-slice_fusion.5
  898.0 1.6 constant_dynamic-slice_fusion.5
  906.4 1.6 constant_dynamic-slice_fusion.5
  914.7 1.6 constant_dynamic-slice_fusion.5
  923.0 1.6 constant_dynamic-slice_fusion.5
  931.3 1.6 constant_dynamic-slice_fusion.5
  934.1 48.2 %all_to_all.18 = bf16[20,64,2,384]{3,2,0,1:T(2,128)(2,1)S(1)} all-to-all(bf16[20,64,2,384]{3,2,0,1:T(2,128)(2,1)} %bitcast.45), channel_id=1, replica_groups=mesh['group'=2,'tm'=4,'bl'=2,'pol'=2] {'tm'}, dimensions={1} | all-to-all | bytes 3932160 | tf_op jit(solution)/shard_map/all_to_all | solution.py:73
  982.4 2.8 copy.11
  (1062 shorter events, 336.0 us)
Async XLA Ops:
  0.0 60.1 %copy-start = (f32[2,16,257]{2,1,0:T(8,128)S(1)}, f32[2,16,257]{2,1,0:T(8,128)}, u32[]{:S(2)}) copy-start(f32[2,16,257]{2,1,0:T(8,128)} %param.9) | copy-start | bytes 98692
  26.2 23.1 %copy-start.2 = (bf16[200,64,2,384]{3,2,1,0:T(2,128)(2,1)}, bf16[200,64,2,384]{3,2,1,0:T(2,128)(2,1)S(1)}, u32[]{:S(2)}) copy-start(bf16[200,64,2,384]{3,2,1,0:T(2,128)(2,1)S(1)} %broadcast_multiply_fusion.1) | copy-start | bytes 58982404
  26.2 33.9 %copy-start.3 = (s32[64]{0:T(128)S(1)}, s32[64]{0:T(128)}, u32[]{:S(2)}) copy-start(s32[64]{0:T(128)} %param.8) | copy-start | bytes 772
  49.3 274.9 %collective-permute-start = (bf16[128,64,2,384]{3,2,1,0:T(2,128)(2,1)}, bf16[128,64,2,384]{3,2,1,0:T(2,128)(2,1)}, u32[]{:S(2)}, u32[]{:S(2)}) collective-permute-start(bf16[128,64,2,384]{3,2,1,0:T(2,128)(2,1)} %get-tuple-element.60), channel_id=1, source_target_pairs={{0,4},{4,8},{8,12},{1,5},{5,9},{9,13},{2,6},{6,10},{10,14},{3,7},{... | collective-permute-start | bytes 37748744 | tf_op jit(solution)/shard_map/ppermute | solution.py:15
  58.8 274.0 %collective-permute-start.1 = (bf16[128,64,2,384]{3,2,1,0:T(2,128)(2,1)}, bf16[128,64,2,384]{3,2,1,0:T(2,128)(2,1)}, u32[]{:S(2)}, u32[]{:S(2)}) collective-permute-start(bf16[128,64,2,384]{3,2,1,0:T(2,128)(2,1)} %get-tuple-element.61), channel_id=1, source_target_pairs={{4,0},{8,4},{12,8},{5,1},{9,5},{13,9},{6,2},{10,6},{14,10},{7,3},{... | collective-permute-start | bytes 37748744 | tf_op jit(solution)/shard_map/ppermute | solution.py:18
  934.1 51.0 %copy-start.1 = (f32[2,16,257]{2,1,0:T(8,128)S(1)}, f32[2,16,257]{2,1,0:T(8,128)}, u32[]{:S(2)}) copy-start(f32[2,16,257]{2,1,0:T(8,128)} %param.9) | copy-start | bytes 98692
where the time goes:
time: 990 us; the launch traced here: 985 us
  local copies, waits for them, and re-layouts  373 us (38%)
  waiting for transfers between devices  272 us (27%)
  loops' own time  136 us (14%)
  other arithmetic  115 us (12%)
  blocking collectives  48.2 us (5%)
  matrix products  29 us (3%)
  starting transfers between devices  10.8 us (1%)
    ppermute x1, waiting for transfers between devices, padded(): lax.ppermute(lax.slice_in_dim(block, block.shape[dim] - width, None, axis...  264 us
    another operation x1, loops' own time, per_device(): lax.map(per_base, jnp.arange(visibilities.shape[1], dtype=jnp.int32))  136 us
    dynamic_slice x64, local copies, waits for them, and re-layouts, per_base(): lax.dynamic_index_in_dim(extended, base_index, 1, False).astype(jnp.float32)  102 us
    another operation x128, local copies, waits for them, and re-layouts, make_band(): jnp.tile(period_row, (1, block_rows))[:, :block_rows * row_width]  78.5 us
    reshape x64, local copies, waits for them, and re-layouts, filter_block(): band_rows.reshape(2, block_rows // AVG, AVG, row_width).sum(axis=2)  73.2 us
    concatenate x1, other arithmetic, padded(): block = jnp.concatenate([low, block, high], axis=dim)  69.3 us
    all_to_all x1, blocking collectives, per_device(): lax.all_to_all(averaged, 'tm', split_axis=1, concat_axis=0, tiled=True)  48.2 us
    dynamic_slice x64, local copies, waits for them, and re-layouts, per_device(): lax.map(per_base, jnp.arange(visibilities.shape[1], dtype=jnp.int32))  41.2 us
  transfers between devices with their start and end apart: 2, of which 2 were waited for; matrix products, arithmetic and copies ran while one was open for 0% of the time, Pallas kernels for 0%

commit v1 on v0

--- a/solution.py
+++ b/solution.py
@@ -70,7 +70,10 @@
 
     filtered = lax.map(per_base, jnp.arange(visibilities.shape[1], dtype=jnp.int32))
     averaged = jnp.moveaxis(filtered, 0, 1).astype(jnp.bfloat16)
-    return lax.all_to_all(averaged, "tm", split_axis=1, concat_axis=0, tiled=True)
+    return jnp.concatenate(
+        lax.all_to_all(jnp.stack(jnp.split(averaged, lax.axis_size("tm"), axis=1)), "tm", 0, 0),
+        axis=0,
+    )
 
 
 def solution(mesh):

time: 990 us -> 1080 us (1.091)
  local copies, waits for them, and re-layouts: 373 us -> 472 us
    dynamic_update_slice x64 -> x128, local copies, waits for them, and re-layouts: 41 us -> 140 us  [per_device(): lax.map(per_base, jnp.arange(visibilities.shape[1], dtype=jnp.int32))]
where the time goes in v1:
time: 1080 us
  local copies, waits for them, and re-layouts  472 us (44%)
  waiting for transfers between devices  272 us (25%)
  loops' own time  130 us (12%)
  other arithmetic  115 us (11%)
  blocking collectives  47 us (4%)
  matrix products  28.9 us (3%)
  starting transfers between devices  10.8 us (1%)
    ppermute x1, waiting for transfers between devices, padded(): lax.ppermute(lax.slice_in_dim(block, block.shape[dim] - width, None, axis...  264 us
    dynamic_update_slice x128, local copies, waits for them, and re-layouts, per_device(): lax.map(per_base, jnp.arange(visibilities.shape[1], dtype=jnp.int32))  140 us
    another operation x1, loops' own time, per_device(): lax.map(per_base, jnp.arange(visibilities.shape[1], dtype=jnp.int32))  130 us
    dynamic_slice x64, local copies, waits for them, and re-layouts, per_base(): lax.dynamic_index_in_dim(extended, base_index, 1, False).astype(jnp.float32)  102 us
    another operation x128, local copies, waits for them, and re-layouts, make_band(): jnp.tile(period_row, (1, block_rows))[:, :block_rows * row_width]  78.5 us
    reshape x64, local copies, waits for them, and re-layouts, filter_block(): band_rows.reshape(2, block_rows // AVG, AVG, row_width).sum(axis=2)  73.2 us
    concatenate x1, other arithmetic, padded(): block = jnp.concatenate([low, block, high], axis=dim)  69.4 us
    all_to_all x1, blocking collectives, per_device(): lax.all_to_all(jnp.stack(jnp.split(averaged, lax.axis_size('tm'), axis=1)...  47 us
  transfers between devices with their start and end apart: 2, of which 2 were waited for; matrix products, arithmetic and copies ran while one was open for 0% of the time, Pallas kernels for 0%

profile of v1, /device:TPU:0, one launch (start us, length us, event | category | flops | bytes accessed | tf_op | source)
XLA Modules:
  0.0 1076.3 jit_solution(120123997905132549)
XLA Ops:
  0.7 25.5 %broadcast_multiply_fusion.1 = bf16[200,64,2,384]{3,2,1,0:T(2,128)(2,1)S(1)} fusion(bf16[200,64,2,384]{3,2,1,0:T(2,128)(2,1)} %param.6, bf16[200]{0:T(256)(128)(2,1)S(1)} %convert_element_type.11), kind=kLoop, calls=%fused_computation.10 | loop fusion | flops 9830400 | bytes 39322000 | tf_op jit(solution)/shard_map/mul | solution.py:61
  26.2 23.0 %fusion.6 = (bf16[128,64,2,384]{3,2,1,0:T(2,128)(2,1)}, bf16[128,64,2,384]{3,2,1,0:T(2,128)(2,1)}) fusion(bf16[200,64,2,384]{3,2,1,0:T(2,128)(2,1)S(1)} %broadcast_multiply_fusion.1), kind=kLoop, calls=%fused_computation.21 | loop fusion | bytes 50331648 | tf_op jit(solution)/shard_map/slice | solution.py:16
  49.3 9.5 collective-permute-start
  60.4 263.7 %collective-permute-done = bf16[128,64,2,384]{3,2,1,0:T(2,128)(2,1)} collective-permute-done((bf16[128,64,2,384]{3,2,1,0:T(2,128)(2,1)}, bf16[128,64,2,384]{3,2,1,0:T(2,128)(2,1)}, u32[]{:S(2)}, u32[]{:S(2)}) %collective-permute-start) | collective-permute-done | bytes 12582944 | tf_op jit(solution)/shard_map/ppermute | solution.py:15
  324.1 8.6 collective-permute-done.1
  332.8 69.4 %pad_maximum_fusion = bf16[456,64,2,384]{3,2,1,0:T(2,128)(2,1)} fusion(bf16[128,64,2,384]{3,2,1,0:T(2,128)(2,1)} %collective-permute-done.1, bf16[200,64,2,384]{3,2,1,0:T(2,128)(2,1)} %copy-done.2, bf16[128,64,2,384]{3,2,1,0:T(2,128)(2,1)} %collective-permute-done), kind=kLoop, calls=%fused_computation.9 | loop fusion | flops 44826624 | bytes 89653248 | tf_op jit(solution)/shard_map/concatenate | solution.py:19
  402.2 622.2 %while.10 = (s32[]{:T(128)}, bf16[64,20,2,384]{3,0,2,1:T(8,128)(2,1)}, s32[64]{0:T(128)S(1)}, f32[64,2,257]{2,0,1:T(8,128)S(1)}, bf16[456,64,2,384]{3,2,1,0:T(2,...) while((s32[]{:T(128)}, bf16[64,20,2,384]{3,0,2,1:T(8,128)(2,1)}, s32[64]{0:T(128)S(1)}, ...), condition=%wide.region_2.3_spmd, body=%wide.region_0.2_spmd.sunk | while | flops 168328320 | bytes 10259991 | solution.py:71
  409.8 2.1 dynamic_update_slice.5
  419.5 2.1 dynamic_update_slice.5
  438.9 2.1 dynamic_update_slice.5
  448.7 2.1 dynamic_update_slice.5
  468.1 2.1 dynamic_update_slice.5
  477.8 2.1 dynamic_update_slice.5
  487.5 2.1 dynamic_update_slice.5
  507.0 2.1 dynamic_update_slice.5
  516.7 2.1 dynamic_update_slice.5
  526.4 2.1 dynamic_update_slice.5
  545.9 2.1 dynamic_update_slice.5
  555.6 2.1 dynamic_update_slice.5
  565.3 2.1 dynamic_update_slice.5
  584.7 2.1 dynamic_update_slice.5
  594.5 2.1 dynamic_update_slice.5
  604.2 2.1 dynamic_update_slice.5
  623.6 2.1 dynamic_update_slice.5
  633.3 2.1 dynamic_update_slice.5
  643.1 2.1 dynamic_update_slice.5
  662.5 2.1 dynamic_update_slice.5
  672.2 2.1 dynamic_update_slice.5
  681.9 2.1 dynamic_update_slice.5
  701.4 2.1 dynamic_update_slice.5
  711.1 2.1 dynamic_update_slice.5
  720.8 2.1 dynamic_update_slice.5
  740.3 2.1 dynamic_update_slice.5
  750.0 2.1 dynamic_update_slice.5
  759.7 2.1 dynamic_update_slice.5
  779.1 2.1 dynamic_update_slice.5
  788.9 2.1 dynamic_update_slice.5
  798.6 2.1 dynamic_update_slice.5
  818.0 2.1 dynamic_update_slice.5
  827.7 2.1 dynamic_update_slice.5
  837.5 2.1 dynamic_update_slice.5
  856.9 2.1 dynamic_update_slice.5
  866.6 2.1 dynamic_update_slice.5
  876.4 2.1 dynamic_update_slice.5
  954.2 2.1 dynamic_update_slice.5
  1022.3 2.1 dynamic_update_slice.5
  1026.5 47.0 %all_to_all.5 = bf16[4,20,16,2,384]{4,2,3,1,0:T(8,128)(2,1)S(1)} all-to-all(bf16[4,20,16,2,384]{4,2,3,1,0:T(8,128)(2,1)S(1)} %pad_maximum_fusion.1), channel_id=1, replica_groups=mesh['group'=2,'tm'=4,'bl'=2,'pol'=2] {'tm'}, dimensions={0} | all-to-all | bytes 3932160 | tf_op jit(solution)/shard_map/all_to_all | solution.py:74
  1073.4 2.8 copy.11
  (1128 shorter events, 413.5 us)
Async XLA Ops:
  0.0 60.1 %copy-start = (f32[2,16,257]{2,1,0:T(8,128)S(1)}, f32[2,16,257]{2,1,0:T(8,128)}, u32[]{:S(2)}) copy-start(f32[2,16,257]{2,1,0:T(8,128)} %param.9) | copy-start | bytes 98692
  26.2 23.1 %copy-start.2 = (bf16[200,64,2,384]{3,2,1,0:T(2,128)(2,1)}, bf16[200,64,2,384]{3,2,1,0:T(2,128)(2,1)S(1)}, u32[]{:S(2)}) copy-start(bf16[200,64,2,384]{3,2,1,0:T(2,128)(2,1)S(1)} %broadcast_multiply_fusion.1) | copy-start | bytes 58982404
  26.2 33.9 %copy-start.3 = (s32[64]{0:T(128)S(1)}, s32[64]{0:T(128)}, u32[]{:S(2)}) copy-start(s32[64]{0:T(128)} %param.8) | copy-start | bytes 772
  49.3 274.9 %collective-permute-start = (bf16[128,64,2,384]{3,2,1,0:T(2,128)(2,1)}, bf16[128,64,2,384]{3,2,1,0:T(2,128)(2,1)}, u32[]{:S(2)}, u32[]{:S(2)}) collective-permute-start(bf16[128,64,2,384]{3,2,1,0:T(2,128)(2,1)} %get-tuple-element.60), channel_id=1, source_target_pairs={{0,4},{4,8},{8,12},{1,5},{5,9},{9,13},{2,6},{6,10},{10,14},{3,7},{... | collective-permute-start | bytes 37748744 | tf_op jit(solution)/shard_map/ppermute | solution.py:15
  58.8 274.0 %collective-permute-start.1 = (bf16[128,64,2,384]{3,2,1,0:T(2,128)(2,1)}, bf16[128,64,2,384]{3,2,1,0:T(2,128)(2,1)}, u32[]{:S(2)}, u32[]{:S(2)}) collective-permute-start(bf16[128,64,2,384]{3,2,1,0:T(2,128)(2,1)} %get-tuple-element.61), channel_id=1, source_target_pairs={{4,0},{8,4},{12,8},{5,1},{9,5},{13,9},{6,2},{10,6},{14,10},{7,3},{... | collective-permute-start | bytes 37748744 | tf_op jit(solution)/shard_map/ppermute | solution.py:18
  1024.4 51.9 %copy-start.1 = (f32[2,16,257]{2,1,0:T(8,128)S(1)}, f32[2,16,257]{2,1,0:T(8,128)}, u32[]{:S(2)}) copy-start(f32[2,16,257]{2,1,0:T(8,128)} %param.9) | copy-start | bytes 98692
